TPU v7x, 32 devices: a whole 2x2x4 slice. The times are simulated.
32 devices in a mesh: fsdp: 16 (over z, x, core), tp: 2 (over y).
Axes of the slice: x: 2, y: 2, z: 4, core: 2. Of those that a mesh axis runs over, the one named last changes fastest.
Arguments:
- tokens: bfloat16 [2048, 3584], P('fsdp', 'tp'), may hold values from -6 to 6
- norm_gain: bfloat16 [3584], replicated, may hold values from 0.5 to 1.5
- gate_weight: bfloat16 [3584, 10240], P('fsdp', 'tp'), may hold values from -0.09375 to 0.09375
- up_weight: bfloat16 [3584, 10240], P('fsdp', 'tp'), may hold values from -0.09375 to 0.09375
- down_weight: bfloat16 [3584, 10240], P('fsdp', 'tp'), may hold values from -0.0625 to 0.0625
- probes: bfloat16 [2, 3584, 10240], P(None, 'fsdp', 'tp'), may hold values from -0.0625 to 0.0625
Outputs:
- layer_out: bfloat16 [2048, 3584], P('tp', 'fsdp')
- token_curv: float32 [2048], P('tp')
All inputs are finite; a program needn't handle non-finite values.
Results may differ from a plain program's by a relative error of at most 0.014.
Values may be sent and summed in bfloat16 or wider, within the bound.
A program may use at most 128 MiB of HBM per device.

v0:
```python
import jax
import jax.numpy as jnp
from jax import lax
from jax.experimental import pallas as pl
from jax.experimental.pallas import tpu as pltpu
from jax.sharding import PartitionSpec as P

D = 3584
PROBES = 2
MESH = pl.DeviceIdType.MESH
ANY = pl.BlockSpec(memory_space=pl.ANY)


epsilon = 1e-06


def remote(src, dst, send, recv, device):
    return pltpu.make_async_remote_copy(
        src_ref=src,
        dst_ref=dst,
        send_sem=send,
        recv_sem=recv,
        device_id=device,
        device_id_type=MESH,
    )


def exchange_kernel(chips, t_ref, g_ref, u_ref, to, go, uo, bounce, t_bounce, w_send, w_recv, c_send, c_recv, t_send, t_recv, local_sem):
    me = lax.axis_index("fsdp")
    tp = lax.axis_index("tp")
    chip, core = me // 2, me % 2
    outer, inner = chip // 2, chip % 2
    outers = chips // 2
    rows, width = go.shape[2], go.shape[3]
    t_rows, t_cols = t_ref.shape
    partner = {"fsdp": chip * 2 + 1 - core}
    across = {"tp": 1 - tp}

    barrier = pltpu.get_barrier_semaphore()
    for d in range(1, chips):
        pl.semaphore_signal(barrier, inc=1, device_id={"fsdp": ((chip + d) % chips) * 2 + core}, device_id_type=MESH)
    pl.semaphore_signal(barrier, inc=1, device_id=partner, device_id_type=MESH)
    pl.semaphore_signal(barrier, inc=1, device_id=across, device_id_type=MESH)
    pl.semaphore_wait(barrier, chips + 1)

    def token_slot(half, owner):
        return to.at[pl.ds(pl.multiple_of(owner * t_rows, t_rows), t_rows), pl.ds(pl.multiple_of(half * t_cols, 128), t_cols)]

    def token_copy(src, half, owner, way, device):
        return remote(src, token_slot(half, owner), t_send.at[way, owner], t_recv.at[half, owner], device)

    down = {"fsdp": (chip - 2) * 2 + core}
    up = {"fsdp": (chip + 2) * 2 + core}
    side = {"fsdp": (outer * 2 + 1 - inner) * 2 + core}

    def pass_on(src, owner, first):
        if first in (0, 1):
            @pl.when(outer > 0)
            def _():
                token_copy(src, tp, owner, 0, down).start()
        if first in (0, 2):
            @pl.when(outer < outers - 1)
            def _():
                token_copy(src, tp, owner, 1, up).start()
        token_copy(src, tp, owner, 2, side).start()
        token_copy(src, tp, owner, 3, across).start()

    pass_on(t_ref, chip, 0)
    weights = ((g_ref, go), (u_ref, uo))
    order = sorted(range(1, chips), key=lambda d: -min(d // 2, (chips - d) // 2))
    sends = [(a, d) for a in range(2) for d in order]

    def weight_send(a, d):
        src, dst = weights[a]
        peer = (chip + d) % chips
        return remote(
            src.at[:, pl.ds(pl.multiple_of(peer * width, 128), width)],
            dst.at[chip, core],
            w_send.at[a, d],
            w_recv.at[a, chip],
            {"fsdp": peer * 2 + core},
        )

    batch = -(-len(sends) // outers)
    batches = [sends[i * batch : (i + 1) * batch] for i in range(outers)]
    for a, d in batches[0]:
        weight_send(a, d).start()

    def own(a):
        return weights[a][0].at[:, pl.ds(pl.multiple_of(chip * width, 128), width)]

    def own_out(a):
        return remote(own(a), weights[a][1].at[chip, core], c_send.at[a, chip], c_recv.at[a, chip], partner)

    for a in range(2):
        own_out(a).start()
        pltpu.make_async_copy(own(a), bounce.at[a], local_sem.at[a]).start()
    pltpu.make_async_copy(t_ref, t_bounce, local_sem.at[2]).start()
    for a in range(2):
        pltpu.make_async_copy(own(a), bounce.at[a], local_sem.at[a]).wait()
        pltpu.make_async_copy(bounce.at[a], weights[a][1].at[chip, core], local_sem.at[a]).start()
    pltpu.make_async_copy(t_ref, t_bounce, local_sem.at[2]).wait()
    pltpu.make_async_copy(t_bounce, token_slot(tp, chip), local_sem.at[2]).start()

    def token_wait(half, owner):
        slot = token_slot(half, owner)
        remote(slot, slot, t_send.at[3, owner], t_recv.at[half, owner], across).wait_recv()

    for r in range(1, outers):
        @pl.when(outer - r >= 0)
        def _():
            owner = chip - 2 * r
            token_wait(tp, owner)
            pass_on(token_slot(tp, owner), owner, 2)

        @pl.when(outer + r < outers)
        def _():
            owner = chip + 2 * r
            token_wait(tp, owner)
            pass_on(token_slot(tp, owner), owner, 1)

        for a, d in batches[r]:
            weight_send(a, d).start()

    def side_owner(z):
        return z * 2 + 1 - inner

    def weight_wait_forward(a, d):
        s = (chip + chips - d) % chips
        block = weights[a][1].at[s, core]
        remote(block, block, w_send.at[a, d], w_recv.at[a, s], partner).wait_recv()
        remote(block, block, c_send.at[a, s], c_recv.at[a, s], partner).start()

    for a, d in batches[0]:
        weight_wait_forward(a, d)
    for z in range(outers):
        owner = side_owner(z)
        token_wait(tp, owner)
        slot = token_slot(tp, owner)
        token_copy(slot, tp, owner, 3, across).start()
    for group in batches[1:]:
        for a, d in group:
            weight_wait_forward(a, d)
    for s in range(chips):
        token_wait(1 - tp, s)
        for a in range(2):
            block = weights[a][1].at[s, 1 - core]
            remote(block, block, c_send.at[a, s], c_recv.at[a, s], partner).wait_recv()

    def sent(owner, way):
        slot = token_slot(tp, owner)
        remote(slot, slot, t_send.at[way, owner], t_recv.at[tp, owner], across).wait_send()

    for a, d in sends:
        weight_send(a, d).wait_send()
    for s in range(chips):
        for a in range(2):
            block = weights[a][1].at[s, core]
            remote(block, block, c_send.at[a, s], c_recv.at[a, s], partner).wait_send()
        sent(s, 3)
    for r in range(outers):
        @pl.when(outer - r >= 0)
        def _():
            owner = chip - 2 * r
            sent(owner, 2)

            @pl.when(outer < outers - 1)
            def _():
                sent(owner, 1)

        @pl.when(outer + r < outers)
        def _():
            owner = chip + 2 * r
            if r > 0:
                sent(owner, 2)

            @pl.when(outer > 0)
            def _():
                sent(owner, 0)
    for a in range(2):
        pltpu.make_async_copy(bounce.at[a], weights[a][1].at[chip, core], local_sem.at[a]).wait()
    pltpu.make_async_copy(t_bounce, token_slot(tp, chip), local_sem.at[2]).wait()


def exchange(tokens, gate_weight, up_weight, chips):
    rows, columns = gate_weight.shape
    width = columns // chips
    t_rows, t_cols = tokens.shape
    weight = jax.ShapeDtypeStruct((chips, 2, rows, width), gate_weight.dtype)
    pieces = pltpu.SemaphoreType.DMA((2, chips))
    t, g, u = pl.pallas_call(
        lambda *refs: exchange_kernel(chips, *refs),
        out_shape=(jax.ShapeDtypeStruct((chips * t_rows, 2 * t_cols), tokens.dtype), weight, weight),
        in_specs=[ANY] * 3,
        out_specs=[ANY] * 3,
        scratch_shapes=[
            pltpu.VMEM((2, rows, width), gate_weight.dtype),
            pltpu.VMEM((t_rows, t_cols), tokens.dtype),
            pieces,
            pieces,
            pieces,
            pieces,
            pltpu.SemaphoreType.DMA((4, chips)),
            pieces,
            pltpu.SemaphoreType.DMA((3,)),
        ],
        compiler_params=pltpu.CompilerParams(collective_id=1, has_side_effects=True),
        name="exchange",
    )(tokens, gate_weight, up_weight)
    return t, g.reshape(-1, width), u.reshape(-1, width)


def project_kernel(chips, h_ref, m0_ref, mp_ref, out_ref, curv_ref, hall, mats, acc, mine, theirs, other, curves, send, recv, c_send, c_recv, y_send, y_recv, v_send, v_recv, local_sem):
    me = lax.axis_index("fsdp")
    tp = lax.axis_index("tp")
    chip, core = me // 2, me % 2
    outer, inner = chip // 2, chip % 2
    outers = chips // 2
    count = h_ref.shape[1]
    last = count - 1
    t_rows, width = h_ref.shape[2], h_ref.shape[3]
    probe_count = mp_ref.shape[0]
    devices = 2 * chips
    partner = {"fsdp": chip * 2 + 1 - core}
    across = {"tp": 1 - tp}
    down = {"fsdp": (chip - 2) * 2 + core}
    up = {"fsdp": (chip + 2) * 2 + core}
    side_chip = outer * 2 + 1 - inner
    side = {"fsdp": side_chip * 2 + core}

    barrier = pltpu.get_barrier_semaphore()
    for d in range(1, devices):
        pl.semaphore_signal(barrier, inc=1, device_id={"fsdp": (me + d) % devices}, device_id_type=MESH)
    pl.semaphore_signal(barrier, inc=1, device_id=across, device_id_type=MESH)
    pl.semaphore_wait(barrier, devices)

    def slot(j, c, k):
        return hall.at[j, c, :, k]

    def hop(src, j, k, way, device):
        return remote(src, slot(j, core, k), send.at[way, k, j], recv.at[k, j], device)

    def relay(src, j, k):
        return remote(src, slot(j, core, k), c_send.at[k, j], c_recv.at[k, j], partner)

    def go_down(src, j, k):
        @pl.when(outer > 0)
        def _():
            hop(src, j, k, 0, down).start()

    def go_up(src, j, k):
        @pl.when(outer < outers - 1)
        def _():
            hop(src, j, k, 1, up).start()

    def arrived(j, k):
        hop(slot(j, core, k), j, k, 2, side).wait_recv()

    hop(h_ref.at[:, last], chip, last, 2, side).start()
    for k in range(count):
        go_down(h_ref.at[:, k], chip, k)
        go_up(h_ref.at[:, k], chip, k)
        if k != last:
            hop(h_ref.at[:, k], chip, k, 2, side).start()
        relay(h_ref.at[:, k], chip, k).start()
    locals_ = [
        pltpu.make_async_copy(h_ref, hall.at[chip, core], local_sem.at[0]),
        pltpu.make_async_copy(m0_ref, mats.at[0], local_sem.at[1]),
        pltpu.make_async_copy(mp_ref, mats.at[pl.ds(1, probe_count)], local_sem.at[2]),
    ]
    for copy in locals_:
        copy.start()
    arrived(side_chip, last)
    go_down(slot(side_chip, core, last), side_chip, last)
    go_up(slot(side_chip, core, last), side_chip, last)
    relay(slot(side_chip, core, last), side_chip, last).start()

    def along(r, k):
        def one(j, onward):
            arrived(j, k)
            block = slot(j, core, k)
            onward(block, j, k)
            if k != last:
                hop(block, j, k, 2, side).start()
            relay(block, j, k).start()

        @pl.when(outer - r >= 0)
        def _():
            one(chip - 2 * r, go_up)
            if k == last:
                one(side_chip - 2 * r, go_up)

        @pl.when(outer + r < outers)
        def _():
            one(chip + 2 * r, go_down)
            if k == last:
                one(side_chip + 2 * r, go_down)

    def sideways(r, k):
        def one(j):
            arrived(j, k)
            relay(slot(j, core, k), j, k).start()

        if r == 0:
            one(side_chip)
        else:
            @pl.when(outer - r >= 0)
            def _():
                one(side_chip - 2 * r)

            @pl.when(outer + r < outers)
            def _():
                one(side_chip + 2 * r)

    def to_across(k):
        return remote(theirs.at[k], other.at[k], y_send.at[k], y_recv.at[k], across)

    def finish(k):
        if k != last:
            sideways(outers - 1, k)
        for j in range(chips):
            block = slot(j, 1 - core, k)
            remote(block, block, c_send.at[k, j], c_recv.at[k, j], partner).wait_recv()
        if k == 0:
            for copy in locals_:
                copy.wait()
        acc[...] = jnp.zeros_like(acc)

        @pl.loop(0, chips)
        def _(j):
            a = hall[j, :, :, k].reshape(4 * t_rows, width)
            for m in range(1 + probe_count):
                acc[m] += lax.dot_general(
                    a,
                    mats[m, :, pl.ds(pl.multiple_of(j * width, 128), width)],
                    (((1,), (1,)), ((), ())),
                    preferred_element_type=jnp.float32,
                )

        def rows(c, half):
            return pl.ds(pl.multiple_of((c * 2 + half) * t_rows, t_rows), t_rows)

        for m in range(1 + probe_count):
            for c in range(2):
                theirs[k, m, pl.ds(c * t_rows, t_rows), :] = acc[m, rows(c, 1 - tp), :].astype(jnp.bfloat16)
        for m in range(1 + probe_count):
            for c in range(2):
                mine[k, m, pl.ds(c * t_rows, t_rows), :] = acc[m, rows(c, tp), :].astype(jnp.bfloat16)
        to_across(k).start()

    def conclude(k):
        to_across(k).wait_recv()

        def total(m):
            return mine[k, m].astype(jnp.float32) + other[k, m].astype(jnp.float32)

        primal = total(0)
        span = pl.ds(k * 2 * t_rows, 2 * t_rows)
        out_ref[span, :] = primal.astype(jnp.bfloat16)
        squashed = jax.nn.sigmoid(primal)
        squares = jnp.zeros_like(primal)
        for m in range(1, 1 + probe_count):
            tangent = total(m)
            squares += tangent * tangent
        terms = squashed * (1.0 - squashed) * squares
        row = lax.dot_general(
            jnp.ones((8, terms.shape[1]), jnp.float32),
            terms,
            (((1,), (1,)), ((), ())),
            precision=lax.Precision.HIGHEST,
            preferred_element_type=jnp.float32,
        )
        curves[me, :, span] = row[0:1, :]

    for r in range(1, outers):
        if r == outers - 1:
            for d in range(max(r - 2, 0), r):
                for k in range(last):
                    sideways(d, k)
        elif r >= 2:
            for k in range(last):
                sideways(r - 2, k)
        for k in range(count):
            along(r, k)
            if r == outers - 1 and k >= 1:
                finish(k - 1)
                if k >= 2:
                    conclude(k - 2)
    finish(last)
    conclude(last - 1)
    conclude(last)

    def curve(owner, d):
        return remote(curves.at[owner], curves.at[owner], v_send.at[d], v_recv.at[owner], {"fsdp": (me + d) % devices})

    for d in range(1, devices):
        curve(me, d).start()

    for k in range(count):
        to_across(k).wait_send()
        for j in range(chips):
            relay(slot(j, core, k), j, k).wait_send()
        if k == last:
            hop(slot(chip, core, k), chip, k, 2, side).wait_send()
        for z in range(outers):
            lanes = [z * 2 + inner]
            if k != last:
                hop(slot(lanes[0], core, k), lanes[0], k, 2, side).wait_send()
            else:
                lanes.append(z * 2 + 1 - inner)
            for j in lanes:
                @pl.when((outer <= z) & (outer > 0))
                def _():
                    hop(slot(j, core, k), j, k, 0, side).wait_send()

                @pl.when((outer >= z) & (outer < outers - 1))
                def _():
                    hop(slot(j, core, k), j, k, 1, side).wait_send()

    for d in range(1, devices):
        curve((me + devices - d) % devices, d).wait_recv()
        curve(me, d).wait_send()
    curv_ref[...] = jnp.sum(curves[...], axis=0) / (PROBES * D)


def project_chunks(hidden, down_weight, probes, chips, t_rows):
    width = hidden.shape[1]
    count = chips // 2
    col_width, columns = down_weight.shape
    kinds = 1 + probes.shape[0]
    kept = count * 2 * t_rows
    hops = pltpu.SemaphoreType.DMA((count, chips))
    part = pltpu.VMEM((count, kinds, 2 * t_rows, col_width), jnp.bfloat16)
    vmem = pl.BlockSpec(memory_space=pltpu.VMEM)
    out, curv = pl.pallas_call(
        lambda *refs: project_kernel(chips, *refs),
        out_shape=(jax.ShapeDtypeStruct((kept, col_width), jnp.bfloat16), jax.ShapeDtypeStruct((1, kept), jnp.float32)),
        in_specs=[ANY] * 3,
        out_specs=[vmem] * 2,
        scratch_shapes=[
            pltpu.VMEM((chips, 2, 2, count, t_rows, width), jnp.bfloat16),
            pltpu.VMEM((kinds, col_width, columns), jnp.bfloat16),
            pltpu.VMEM((kinds, 4 * t_rows, col_width), jnp.float32),
            part,
            part,
            part,
            pltpu.VMEM((2 * chips, 1, kept), jnp.float32),
            pltpu.SemaphoreType.DMA((3, count, chips)),
            hops,
            hops,
            hops,
            pltpu.SemaphoreType.DMA((count,)),
            pltpu.SemaphoreType.DMA((count,)),
            pltpu.SemaphoreType.DMA((2 * chips,)),
            pltpu.SemaphoreType.DMA((2 * chips,)),
            pltpu.SemaphoreType.DMA((3,)),
        ],
        compiler_params=pltpu.CompilerParams(collective_id=2, has_side_effects=True, vmem_limit_bytes=56 * 2**20),
        name="project",
    )(hidden.reshape(2, count, t_rows, width), down_weight, probes)
    return out, curv.reshape(kept)


def norm(features, norm_gain):
    widened = features.astype(jnp.float32)
    inverse_rms = lax.rsqrt(jnp.mean(widened * widened, axis=1, keepdims=True) + epsilon)
    return (widened * inverse_rms * norm_gain.astype(jnp.float32)).astype(jnp.bfloat16)


def dot(a, b):
    return jnp.dot(a, b, preferred_element_type=jnp.float32)


def project(hidden_all, down_weight, probes):
    stacked = jnp.concatenate([down_weight[None], probes], axis=0)
    count = stacked.shape[0]
    col_width = stacked.shape[1]
    flat_weights = stacked.reshape(count * col_width, stacked.shape[2])
    partial_terms = lax.dot_general(
        hidden_all,
        flat_weights,
        (((1,), (1,)), ((), ())),
        preferred_element_type=jnp.float32,
    )
    summed = lax.psum_scatter(
        partial_terms.astype(jnp.bfloat16), "tp", scatter_dimension=0, tiled=True
    ).astype(jnp.float32)
    summed_parts = summed.reshape(summed.shape[0], count, col_width)
    primal = summed_parts[:, 0, :]
    tangents = summed_parts[:, 1:, :]
    squashed = jax.nn.sigmoid(primal)
    slope = squashed * (1.0 - squashed)
    tangent_sq = jnp.sum(tangents * tangents, axis=1)
    local_curv = jnp.sum(slope * tangent_sq, axis=1) / (PROBES * D)
    token_curv = lax.psum(local_curv, "fsdp")
    return (primal.astype(jnp.bfloat16), token_curv)


def gathered_weights(tokens, norm_gain, gate_weight, up_weight, down_weight, probes):
    normed = norm(lax.all_gather(tokens, "tp", axis=1, tiled=True), norm_gain)
    gate_sum = dot(normed, lax.all_gather(gate_weight, "fsdp", axis=0, tiled=True))
    up_sum = dot(normed, lax.all_gather(up_weight, "fsdp", axis=0, tiled=True))
    hidden = (jax.nn.silu(gate_sum) * up_sum).astype(jnp.bfloat16)
    return project(lax.all_gather(hidden, "fsdp", axis=0, tiled=True), down_weight, probes)


def moved_weights(tokens, norm_gain, gate_weight, up_weight, down_weight, probes):
    chips = lax.axis_size("fsdp") // 2
    features, gate, up = exchange(tokens, gate_weight, up_weight, chips)
    normed = norm(features, norm_gain)
    hidden = (jax.nn.silu(dot(normed, gate)) * dot(normed, up)).astype(jnp.bfloat16)
    return project_chunks(hidden, down_weight, probes, chips, tokens.shape[0])


def solution(mesh):
    def on_device(tokens, norm_gain, gate_weight, up_weight, down_weight, probes):
        chips = mesh.shape["fsdp"] // 2
        fits = mesh.shape["tp"] == 2 and chips % 2 == 0 and gate_weight.shape[1] % (128 * chips) == 0 and tokens.shape[1] % 128 == 0
        form = moved_weights if fits else gathered_weights
        return form(tokens, norm_gain, gate_weight, up_weight, down_weight, probes)

    return jax.shard_map(
        on_device,
        mesh=mesh,
        in_specs=(
            P("fsdp", "tp"),
            P(),
            P("fsdp", "tp"),
            P("fsdp", "tp"),
            P("fsdp", "tp"),
            P(None, "fsdp", "tp"),
        ),
        out_specs=(P("tp", "fsdp"), P("tp")),
        check_vma=False,
    )
```

profile of v0, /device:TPU:0, one launch (start us, length us, event | category | flops | bytes accessed | tf_op | source)
XLA Modules:
  0.0 352.6 jit_solution(17202500280435351450)
XLA Ops:
  0.6 0.7 convert_element_type.13
  1.3 149.4 %exchange.1 = (bf16[1024,3584]{1,0:T(8,128)(2,1)}, bf16[8,2,224,640]{3,2,1,0:T(8,128)(2,1)}, bf16[8,2,224,640]{3,2,1,0:T(8,128)(2,1)}) custom-call(bf16[128,1792]{1,0:T(8,128)(2,1)} %refs_0_.1, bf16[224,5120]{1,0:T(8,128)(2,1)} %refs_1_.2, bf16[224,5120]{1,0:T(8,128)(2,1)} %refs_2_.2), custom_call_target="tpu_custom_call" | custom-call | tf_op jit(solution)/shard_map/exchange/pallas_call | solution.py:191
  150.7 0.0 copy-start
  150.7 0.0 slice-start
  150.7 4.7 %fusion = f32[1024]{0:T(1024)S(1)} fusion(bf16[1024,3584]{1,0:T(8,128)(2,1)} %get-tuple-element.7), kind=kLoop, calls=%fused_computation.2 | loop fusion | flops 11009024 | bytes 7344128 | tf_op jit(solution)/shard_map/reduce_sum | solution.py:466
  155.5 0.4 copy-done
  155.9 0.0 slice-start.1
  155.9 8.3 %fusion.3 = f32[1024,640]{1,0:T(8,128)S(1)} fusion(bf16[3584,640]{1,0:T(8,128)(2,1)} %bitcast.11, bf16[1024,3584]{1,0:T(8,128)(2,1)S(1)} %copy-done, f32[3584]{0:T(1024)S(1)} %convert_element_type.13, f32[1024]{0:T(1024)S(1)} %add_rsqrt_fusion), kind=kOutput, calls=%fused_computation.6 | convolution fusion | flops 4712300544 | bytes 14567424 | tf_op jit(solution)/shard_map/dot_general | solution.py:471
  164.2 0.0 slice-done
  164.2 0.0 slice-done.1
  164.2 7.2 %multiply_convert_fusion = bf16[1024,640]{1,0:T(8,128)(2,1)} fusion(f32[1024,640]{1,0:T(8,128)S(1)} %fusion.3, bf16[3584,640]{1,0:T(8,128)(2,1)S(1)} %bitcast.10, bf16[1024,3584]{1,0:T(8,128)(2,1)S(1)} %copy-done, f32[3584]{0:T(1024)S(1)} %convert_element_type.13, f32[1024]{0:T(1024)S(1)} %add_rsqrt_fusion), kind=kOutput, calls=%fused_computation.5 | convolution fusion | flops 4716232704 | bytes 15878144 | tf_op jit(solution)/shard_map/dot_general | solution.py:471
  171.4 177.9 %project.1 = (bf16[1024,224]{1,0:T(8,128)(2,1)}, f32[1,1024]{1,0:T(1,128)}) custom-call(bf16[2,4,128,640]{3,2,1,0:T(8,128)(2,1)} %bitcast.6, bf16[224,5120]{1,0:T(8,128)(2,1)} %refs_1_.3, bf16[2,224,5120]{2,1,0:T(8,128)(2,1)} %refs_2_.3), custom_call_target="tpu_custom_call" | custom-call | tf_op jit(solution)/shard_map/project/pallas_call | solution.py:435
  349.3 2.0 copy.8
  351.3 1.3 copy.10
  (2 shorter events, 0.0 us)
Async XLA Ops:
  150.7 5.2 %copy-start = (bf16[1024,3584]{1,0:T(8,128)(2,1)S(1)}, bf16[1024,3584]{1,0:T(8,128)(2,1)}, u32[]{:S(2)}) copy-start(bf16[1024,3584]{1,0:T(8,128)(2,1)} %get-tuple-element.7) | copy-start | bytes 22020100
  150.7 13.5 %slice-start = ((s8[4587520]{0:T(1024)(128)(4,1)}), s8[393216]{0:T(1024)(128)(4,1)S(1)}, s32[]{:S(2)}) async-start(s8[4587520]{0:T(1024)(128)(4,1)} %bitcast.8), calls=%async_computation | async-start | bytes 786432
  155.9 8.4 %slice-start.1 = ((s8[4587520]{0:T(1024)(128)(4,1)}), s8[4194304]{0:T(1024)(128)(4,1)S(1)}, s32[]{:S(2)}) async-start(s8[4587520]{0:T(1024)(128)(4,1)} %bitcast.8), calls=%async_computation.1 | async-start | bytes 8388608
where the time goes:
time: 353 us
  Pallas kernels  327 us (93%)
  matrix products  15.5 us (4%)
  other arithmetic  5.44 us (2%)
  local copies, waits for them, and re-layouts  3.7 us (1%)
    pallas_call x1, Pallas kernels, project_chunks(): pl.pallas_call(lambda *refs: project_kernel(chips, *refs), out_shape=(jax...  178 us
    pallas_call x1, Pallas kernels, exchange(): pl.pallas_call(lambda *refs: exchange_kernel(chips, *refs), out_shape=(ja...  149 us
    dot_general x2, matrix products, dot(): return jnp.dot(a, b, preferred_element_type=jnp.float32)  15.5 us

commit v1 on v0

v1 whole, which is shorter than its diff:
```python
import jax
import jax.numpy as jnp
from jax import lax
from jax.experimental import pallas as pl
from jax.experimental.pallas import tpu as pltpu
from jax.sharding import PartitionSpec as P

D = 3584
PROBES = 2
MESH = pl.DeviceIdType.MESH
ANY = pl.BlockSpec(memory_space=pl.ANY)


epsilon = 1e-06


def remote(src, dst, send, recv, device):
    return pltpu.make_async_remote_copy(
        src_ref=src,
        dst_ref=dst,
        send_sem=send,
        recv_sem=recv,
        device_id=device,
        device_id_type=MESH,
    )


def fused_kernel(chips, t_ref, gain_ref, g_ref, u_ref, m0_ref, mp_ref, out_ref, curv_ref, tok, wts, hall, mats, acc, mine, theirs, other, curves,
                 t_send, t_recv, w_send, w_recv, wc_send, wc_recv, z_send, x_send, h_recv, c_send, c_recv, y_send, y_recv, v_send, v_recv, local_sem):
    me = lax.axis_index("fsdp")
    tp = lax.axis_index("tp")
    chip, core = me // 2, me % 2
    outer, inner = chip // 2, chip % 2
    outers = chips // 2
    devices = 2 * chips
    owners = chips // 2
    parts, t_rows, t_cols = t_ref.shape
    rows = g_ref.shape[0]
    count = hall.shape[0]
    width = hall.shape[-1]
    kinds, col_width = 1 + mp_ref.shape[0], m0_ref.shape[0]
    side_chip = outer * 2 + 1 - inner
    partner = {"fsdp": chip * 2 + 1 - core}
    across = {"tp": 1 - tp}
    down = {"fsdp": (chip - 2) * 2 + core}
    up = {"fsdp": (chip + 2) * 2 + core}
    side = {"fsdp": side_chip * 2 + core}
    features = chips * 2 * rows

    barrier = pltpu.get_barrier_semaphore()
    for d in range(1, devices):
        pl.semaphore_signal(barrier, inc=1, device_id={"fsdp": (me + d) % devices}, device_id_type=MESH)
    pl.semaphore_signal(barrier, inc=1, device_id=across, device_id_type=MESH)
    pl.semaphore_wait(barrier, devices)

    def token_slot(half, owner):
        return tok.at[owner, :, :, pl.ds(pl.multiple_of(half * t_cols, 128), t_cols)]

    def token_copy(src, half, owner, way, device):
        return remote(src, token_slot(half, owner), t_send.at[way, owner], t_recv.at[half, owner], device)

    def pass_on(src, owner, first):
        if first in (0, 1):
            @pl.when(outer > 0)
            def _():
                token_copy(src, tp, owner, 0, down).start()
        if first in (0, 2):
            @pl.when(outer < outers - 1)
            def _():
                token_copy(src, tp, owner, 1, up).start()
        token_copy(src, tp, owner, 2, side).start()
        token_copy(src, tp, owner, 3, across).start()

    def token_wait(half, owner):
        slot = token_slot(half, owner)
        remote(slot, slot, t_send.at[3, owner], t_recv.at[half, owner], across).wait_recv()

    weights = (g_ref, u_ref)

    def piece(a, owner):
        return weights[a].at[:, pl.ds(pl.multiple_of(owner * width, 128), width)]

    def landing(a, source, c):
        return wts.at[source, c, :, pl.ds(a * width, width)]

    def weight_send(a, peer):
        return remote(piece(a, peer), landing(a, chip, core), w_send.at[a, peer], w_recv.at[a, chip], {"fsdp": peer * 2 + core})

    def weight_pass(a, source):
        block = landing(a, source, core)
        return remote(block, block, wc_send.at[a, source], wc_recv.at[a, source], partner)

    def line(base, step, act):
        for d in range(outers - 1, 0, -1):
            @pl.when((outer + step * d >= 0) & (outer + step * d < outers))
            def _():
                for a in range(2):
                    act(a, base + 2 * step * d)

    def start_send(a, peer):
        weight_send(a, peer).start()

    def weights_along(r):
        @pl.when(outer == r)
        def _():
            line(chip, 1, start_send)

        @pl.when(outer == outers - 1 - r)
        def _():
            line(chip, -1, start_send)

    pass_on(t_ref, chip, 0)
    weights_along(0)
    own_out = [remote(piece(a, chip), landing(a, chip, core), wc_send.at[a, chip], wc_recv.at[a, chip], partner) for a in range(2)]
    locals_ = [pltpu.make_async_copy(piece(a, chip), landing(a, chip, core), local_sem.at[a]) for a in range(2)]
    locals_ += [
        pltpu.make_async_copy(t_ref, token_slot(tp, chip), local_sem.at[2]),
        pltpu.make_async_copy(m0_ref, mats.at[0], local_sem.at[3]),
        pltpu.make_async_copy(mp_ref, mats.at[pl.ds(1, kinds - 1)], local_sem.at[4]),
    ]
    for copy in own_out + locals_:
        copy.start()

    for r in range(1, outers):
        @pl.when(outer - r >= 0)
        def _():
            owner = chip - 2 * r
            token_wait(tp, owner)
            pass_on(token_slot(tp, owner), owner, 2)

        @pl.when(outer + r < outers)
        def _():
            owner = chip + 2 * r
            token_wait(tp, owner)
            pass_on(token_slot(tp, owner), owner, 1)

        weights_along(r)
    line(side_chip, 1, start_send)
    line(side_chip, -1, start_send)
    for a in range(2):
        start_send(a, side_chip)

    for z in range(outers):
        owner = z * 2 + 1 - inner
        token_wait(tp, owner)
        token_copy(token_slot(tp, owner), tp, owner, 3, across).start()

    def take(a, source):
        block = landing(a, source, core)
        remote(block, block, w_send.at[a, source], w_recv.at[a, source], partner).wait_recv()
        weight_pass(a, source).start()

    line(chip, 1, take)
    line(chip, -1, take)
    for a in range(2):
        take(a, side_chip)
    line(side_chip, 1, take)
    line(side_chip, -1, take)
    for s in range(chips):
        token_wait(1 - tp, s)
    for s in range(chips):
        for a in range(2):
            block = landing(a, s, 1 - core)
            remote(block, block, wc_send.at[a, s], wc_recv.at[a, s], partner).wait_recv()
    for copy in locals_:
        copy.wait()

    def hidden(k):
        o, s = k // parts, k % parts

        def normed(owner):
            widened = tok[owner, s].astype(jnp.float32)
            inverse_rms = lax.rsqrt(jnp.mean(widened * widened, axis=1, keepdims=True) + epsilon)
            return (widened * inverse_rms * gain_ref[...].astype(jnp.float32)).astype(jnp.bfloat16)

        left = jnp.concatenate([normed(o), normed(owners + o)], axis=0)
        sums = jnp.dot(left, wts[...].reshape(features, 2 * width), preferred_element_type=jnp.float32)
        values = (jax.nn.silu(sums[:, :width]) * sums[:, width:]).astype(jnp.bfloat16)
        hall[k, chip, core, 0] = values[:t_rows]
        hall[k, chip, core, 1] = values[t_rows:]

    def block_of(k, j):
        return hall.at[k, j, core]

    def along(k, j, way):
        block = block_of(k, j)
        return remote(block, block, z_send.at[way, k, j], h_recv.at[k, j], (down, up)[way])

    def sideways(k, j):
        block = block_of(k, j)
        return remote(block, block, x_send.at[k, j], h_recv.at[k, j], side)

    def relay(k, j):
        block = block_of(k, j)
        return remote(block, block, c_send.at[k, j], c_recv.at[k, j], partner)

    def arrived(k, j):
        sideways(k, j).wait_recv()

    def go(k, j, way):
        @pl.when((outer > 0) if way == 0 else (outer < outers - 1))
        def _():
            along(k, j, way).start()

    def doubled(k, z):
        return (k % 2 == 1) & ((z == 0) | (z == outers - 1))

    def inject(k):
        for way in range(2):
            go(k, chip, way)
        sideways(k, chip).start()
        relay(k, chip).start()

    def hop(k, r, way):
        z = outer - r if way else outer + r

        @pl.when((z >= 0) & (z < outers))
        def _():
            j = z * 2 + inner
            arrived(k, j)
            go(k, j, way)

            @pl.when(jnp.logical_not(doubled(k, z)))
            def _():
                sideways(k, j).start()

            relay(k, j).start()

    def beside(k, d):
        def one(z, way):
            @pl.when((z >= 0) & (z < outers))
            def _():
                j = z * 2 + 1 - inner
                arrived(k, j)
                if d == 0:
                    @pl.when(doubled(k, z))
                    def _():
                        for w in range(2):
                            go(k, j, w)
                else:
                    @pl.when(doubled(k, z))
                    def _():
                        go(k, j, way)

                relay(k, j).start()

        one(outer - d, 1)
        if d:
            one(outer + d, 0)

    def to_across(k):
        return remote(theirs.at[k], other.at[k], y_send.at[k], y_recv.at[k], across)

    def finish(k):
        for j in range(chips):
            block = hall.at[k, j, 1 - core]
            remote(block, block, c_send.at[k, j], c_recv.at[k, j], partner).wait_recv()
        acc[...] = jnp.zeros_like(acc)

        @pl.loop(0, chips // 2)
        def _(p):
            right = jnp.concatenate(
                [jnp.concatenate([hall[k, 2 * p, c, half], hall[k, 2 * p + 1, c, half]], axis=1) for half in range(2) for c in range(2)],
                axis=0,
            )
            left = mats[:, :, pl.ds(pl.multiple_of(p * 2 * width, 128), 2 * width)].reshape(kinds * col_width, 2 * width)
            acc[...] += lax.dot_general(left, right, (((1,), (1,)), ((), ())), preferred_element_type=jnp.float32)

        def lanes(half):
            return pl.ds(pl.multiple_of(half * 2 * t_rows, 128), 2 * t_rows)

        theirs[k] = acc[:, lanes(1 - tp)].astype(jnp.bfloat16)
        mine[k] = acc[:, lanes(tp)].astype(jnp.bfloat16)
        to_across(k).start()

    def conclude(k):
        to_across(k).wait_recv()

        def total(m):
            span = pl.ds(m * col_width, col_width)
            return mine[k, span, :].astype(jnp.float32) + other[k, span, :].astype(jnp.float32)

        primal = total(0)
        squashed = jax.nn.sigmoid(primal)
        squares = jnp.zeros_like(primal)
        for m in range(1, kinds):
            tangent = total(m)
            squares += tangent * tangent
        terms = squashed * (1.0 - squashed) * squares
        curves[me, pl.ds(k, 1), :] = jnp.sum(terms, axis=0, keepdims=True)
        fill = -col_width % 128
        turned = jnp.concatenate([primal, jnp.zeros((fill, 2 * t_rows), jnp.float32)], axis=0).T.astype(jnp.bfloat16)
        o, s = k // parts, k % parts
        for c in range(2):
            span = pl.ds(pl.multiple_of(((o * 2 + c) * parts + s) * t_rows, t_rows), t_rows)
            out_ref[span, :] = turned[c * t_rows : (c + 1) * t_rows, :col_width]

    lag = outers

    @pl.loop(0, count + lag)
    def _(i):
        @pl.when(i < count)
        def _():
            hidden(i)
            inject(i)

        for r in range(1, outers):
            @pl.when((i - r >= 0) & (i - r < count))
            def _():
                hop(i - r, r, 0)
                hop(i - r, r, 1)

        for d in range(outers):
            @pl.when((i - d - 1 >= 0) & (i - d - 1 < count))
            def _():
                beside(i - d - 1, d)

        @pl.when((i - lag >= 0) & (i - lag < count))
        def _():
            finish(i - lag)

        @pl.when((i - lag - 1 >= 0) & (i - lag - 1 < count))
        def _():
            conclude(i - lag - 1)

    conclude(count - 1)

    def curve(owner, d):
        return remote(curves.at[owner], curves.at[owner], v_send.at[d], v_recv.at[owner], {"fsdp": (me + d) % devices})

    for d in range(1, devices):
        curve(me, d).start()

    def drop(a, peer):
        weight_send(a, peer).wait_send()

    for base in (chip, side_chip):
        line(base, 1, drop)
        line(base, -1, drop)
    for a in range(2):
        drop(a, side_chip)
    for copy in own_out:
        copy.wait_send()
    for a in range(2):
        for s in range(chips):
            @pl.when(s != chip)
            def _():
                weight_pass(a, s).wait_send()

    def sent(owner, way):
        slot = token_slot(tp, owner)
        remote(slot, slot, t_send.at[way, owner], t_recv.at[tp, owner], across).wait_send()

    for s in range(chips):
        sent(s, 3)
    for r in range(outers):
        @pl.when(outer - r >= 0)
        def _():
            owner = chip - 2 * r
            sent(owner, 2)

            @pl.when(outer < outers - 1)
            def _():
                sent(owner, 1)

        @pl.when(outer + r < outers)
        def _():
            owner = chip + 2 * r
            if r > 0:
                sent(owner, 2)

            @pl.when(outer > 0)
            def _():
                sent(owner, 0)

    @pl.loop(0, count)
    def _(k):
        to_across(k).wait_send()
        for j in range(chips):
            relay(k, j).wait_send()
        for z in range(outers):
            j = z * 2 + inner
            twin = z * 2 + 1 - inner
            twice = doubled(k, z)

            @pl.when((z == outer) | jnp.logical_not(twice))
            def _():
                sideways(k, j).wait_send()

            def went(way):
                along(k, j, way).wait_send()

                @pl.when(twice)
                def _():
                    along(k, twin, way).wait_send()

            @pl.when((outer <= z) & (outer > 0))
            def _():
                went(0)

            @pl.when((outer >= z) & (outer < outers - 1))
            def _():
                went(1)

    for d in range(1, devices):
        curve((me + devices - d) % devices, d).wait_recv()
        curve(me, d).wait_send()
    curv_ref[...] = jnp.sum(curves[...], axis=0) / (PROBES * D)


def fused(tokens, norm_gain, gate_weight, up_weight, down_weight, probes, chips):
    t_all, t_cols = tokens.shape
    parts = 2 if t_all % 128 == 0 else 1
    t_rows = t_all // parts
    rows, columns = gate_weight.shape
    width = columns // chips
    col_width, span = down_weight.shape
    kinds = 1 + probes.shape[0]
    count = parts * chips // 2
    kept = count * 2 * t_rows
    pieces = pltpu.SemaphoreType.DMA((2, chips))
    hops = pltpu.SemaphoreType.DMA((count, chips))
    part = pltpu.VMEM((count, kinds * col_width, 2 * t_rows), jnp.bfloat16)
    vmem = pl.BlockSpec(memory_space=pltpu.VMEM)
    out, curv = pl.pallas_call(
        lambda *refs: fused_kernel(chips, *refs),
        out_shape=(jax.ShapeDtypeStruct((kept, col_width), jnp.bfloat16), jax.ShapeDtypeStruct((count, 2 * t_rows), jnp.float32)),
        in_specs=[ANY, vmem, ANY, ANY, ANY, ANY],
        out_specs=[vmem] * 2,
        scratch_shapes=[
            pltpu.VMEM((chips, parts, t_rows, 2 * t_cols), jnp.bfloat16),
            pltpu.VMEM((chips, 2, rows, 2 * width), jnp.bfloat16),
            pltpu.VMEM((count, chips, 2, 2, t_rows, width), jnp.bfloat16),
            pltpu.VMEM((kinds, col_width, span), jnp.bfloat16),
            pltpu.VMEM((kinds * col_width, 4 * t_rows), jnp.float32),
            part,
            part,
            part,
            pltpu.VMEM((2 * chips, count, 2 * t_rows), jnp.float32),
            pltpu.SemaphoreType.DMA((4, chips)),
            pieces,
            pieces,
            pieces,
            pieces,
            pieces,
            pltpu.SemaphoreType.DMA((2, count, chips)),
            hops,
            hops,
            hops,
            hops,
            pltpu.SemaphoreType.DMA((count,)),
            pltpu.SemaphoreType.DMA((count,)),
            pltpu.SemaphoreType.DMA((2 * chips,)),
            pltpu.SemaphoreType.DMA((2 * chips,)),
            pltpu.SemaphoreType.DMA((5,)),
        ],
        compiler_params=pltpu.CompilerParams(collective_id=1, has_side_effects=True, vmem_limit_bytes=63 * 2**20),
        name="fused",
    )(tokens.reshape(parts, t_rows, t_cols), norm_gain.reshape(1, -1), gate_weight, up_weight, down_weight, probes)
    curv = curv.reshape(count // parts, parts, 2, t_rows).transpose(0, 2, 1, 3)
    return out, curv.reshape(kept)


def norm(features, norm_gain):
    widened = features.astype(jnp.float32)
    inverse_rms = lax.rsqrt(jnp.mean(widened * widened, axis=1, keepdims=True) + epsilon)
    return (widened * inverse_rms * norm_gain.astype(jnp.float32)).astype(jnp.bfloat16)


def dot(a, b):
    return jnp.dot(a, b, preferred_element_type=jnp.float32)


def project(hidden_all, down_weight, probes):
    stacked = jnp.concatenate([down_weight[None], probes], axis=0)
    count = stacked.shape[0]
    col_width = stacked.shape[1]
    flat_weights = stacked.reshape(count * col_width, stacked.shape[2])
    partial_terms = lax.dot_general(
        hidden_all,
        flat_weights,
        (((1,), (1,)), ((), ())),
        preferred_element_type=jnp.float32,
    )
    summed = lax.psum_scatter(
        partial_terms.astype(jnp.bfloat16), "tp", scatter_dimension=0, tiled=True
    ).astype(jnp.float32)
    summed_parts = summed.reshape(summed.shape[0], count, col_width)
    primal = summed_parts[:, 0, :]
    tangents = summed_parts[:, 1:, :]
    squashed = jax.nn.sigmoid(primal)
    slope = squashed * (1.0 - squashed)
    tangent_sq = jnp.sum(tangents * tangents, axis=1)
    local_curv = jnp.sum(slope * tangent_sq, axis=1) / (PROBES * D)
    token_curv = lax.psum(local_curv, "fsdp")
    return (primal.astype(jnp.bfloat16), token_curv)


def gathered_weights(tokens, norm_gain, gate_weight, up_weight, down_weight, probes):
    normed = norm(lax.all_gather(tokens, "tp", axis=1, tiled=True), norm_gain)
    gate_sum = dot(normed, lax.all_gather(gate_weight, "fsdp", axis=0, tiled=True))
    up_sum = dot(normed, lax.all_gather(up_weight, "fsdp", axis=0, tiled=True))
    hidden = (jax.nn.silu(gate_sum) * up_sum).astype(jnp.bfloat16)
    return project(lax.all_gather(hidden, "fsdp", axis=0, tiled=True), down_weight, probes)


def moved_weights(tokens, norm_gain, gate_weight, up_weight, down_weight, probes):
    chips = lax.axis_size("fsdp") // 2
    return fused(tokens, norm_gain, gate_weight, up_weight, down_weight, probes, chips)


def solution(mesh):
    def on_device(tokens, norm_gain, gate_weight, up_weight, down_weight, probes):
        chips = mesh.shape["fsdp"] // 2
        fits = mesh.shape["tp"] == 2 and chips % 2 == 0 and gate_weight.shape[1] % (128 * chips) == 0 and tokens.shape[1] % 128 == 0
        form = moved_weights if fits else gathered_weights
        return form(tokens, norm_gain, gate_weight, up_weight, down_weight, probes)

    return jax.shard_map(
        on_device,
        mesh=mesh,
        in_specs=(
            P("fsdp", "tp"),
            P(),
            P("fsdp", "tp"),
            P("fsdp", "tp"),
            P("fsdp", "tp"),
            P(None, "fsdp", "tp"),
        ),
        out_specs=(P("tp", "fsdp"), P("tp")),
        check_vma=False,
    )
```

time: 353 us -> 272 us (0.77)
  Pallas kernels: 327 us -> 266 us
  matrix products: 15.5 us -> 0 us
  other arithmetic: 5.44 us -> 0 us
    pallas_call x2 -> x1, Pallas kernels: 327 us -> 266 us  [fused(): pl.pallas_call(lambda *refs: fused_kernel(chips, *refs), out_shape=(jax.S...]
    dot_general x2 -> x0, matrix products: 15.5 us -> none  [dot(): return jnp.dot(a, b, preferred_element_type=jnp.float32)]
    reduce_sum x1 -> x0, other arithmetic: 4.73 us -> none  [norm(): jnp.mean(widened * widened, axis=1, keepdims=True) + epsilon]
where the time goes in v1:
time: 272 us
  Pallas kernels  266 us (98%)
  local copies, waits for them, and re-layouts  4.74 us (2%)
    pallas_call x1, Pallas kernels, fused(): pl.pallas_call(lambda *refs: fused_kernel(chips, *refs), out_shape=(jax.S...  266 us

profile of v1, /device:TPU:0, one launch (start us, length us, event | category | flops | bytes accessed | tf_op | source)
XLA Modules:
  0.0 271.7 jit_solution(2148846378693050454)
XLA Ops:
  0.6 1.3 reshape.17.refs_1_
  1.9 266.3 %fused.1 = (bf16[1024,224]{1,0:T(8,128)(2,1)}, f32[8,128]{1,0:T(8,128)}) custom-call(bf16[2,64,1792]{2,1,0:T(8,128)(2,1)} %bitcast.4, bf16[1,3584]{1,0:T(2,128)(2,1)} %reshape.17.refs_1_, bf16[224,5120]{1,0:T(8,128)(2,1)} %refs_2_.1, bf16[224,5120]{1,0:T(8,128)(2,1)} %refs_3_.1, bf16[224,5120]{1,0:T(8,128)(2,1)} %refs_4_.1, bf16[2,224,5120]{2,1,0:T(8,128)(2,1)} %refs_5_.1), custom_call_target="tpu_custom_call" | custom-call | tf_op jit(solution)/shard_map/fused/pallas_call | solution.py:425
  268.3 2.0 copy.10
  270.3 0.7 reshape.18
  271.1 0.7 reshape.19
  (1 shorter events, 0.0 us)

commit v2 on v1

--- a/solution.py
+++ b/solution.py
@@ -104,12 +104,16 @@
         @pl.when(outer == r)
         def _():
             line(chip, 1, start_send)
+            line(side_chip, 1, start_send)
 
         @pl.when(outer == outers - 1 - r)
         def _():
             line(chip, -1, start_send)
+            line(side_chip, -1, start_send)
 
     pass_on(t_ref, chip, 0)
+    for a in range(2):
+        start_send(a, side_chip)
     weights_along(0)
     own_out = [remote(piece(a, chip), landing(a, chip, core), wc_send.at[a, chip], wc_recv.at[a, chip], partner) for a in range(2)]
     locals_ = [pltpu.make_async_copy(piece(a, chip), landing(a, chip, core), local_sem.at[a]) for a in range(2)]
@@ -135,10 +139,6 @@
             pass_on(token_slot(tp, owner), owner, 1)
 
         weights_along(r)
-    line(side_chip, 1, start_send)
-    line(side_chip, -1, start_send)
-    for a in range(2):
-        start_send(a, side_chip)
 
     for z in range(outers):
         owner = z * 2 + 1 - inner
@@ -157,8 +157,6 @@
     line(side_chip, 1, take)
     line(side_chip, -1, take)
     for s in range(chips):
-        token_wait(1 - tp, s)
-    for s in range(chips):
         for a in range(2):
             block = landing(a, s, 1 - core)
             remote(block, block, wc_send.at[a, s], wc_recv.at[a, s], partner).wait_recv()
@@ -167,6 +165,11 @@
 
     def hidden(k):
         o, s = k // parts, k % parts
+
+        @pl.when(s == 0)
+        def _():
+            token_wait(1 - tp, o)
+            token_wait(1 - tp, owners + o)
 
         def normed(owner):
             widened = tok[owner, s].astype(jnp.float32)

time: 272 us -> 259 us (0.952)
  Pallas kernels: 266 us -> 254 us
    pallas_call x1, Pallas kernels: 266 us -> 254 us  [fused(): pl.pallas_call(lambda *refs: fused_kernel(chips, *refs), out_shape=(jax.S...]
where the time goes in v2:
time: 259 us
  Pallas kernels  254 us (98%)
  local copies, waits for them, and re-layouts  4.74 us (2%)
    pallas_call x1, Pallas kernels, fused(): pl.pallas_call(lambda *refs: fused_kernel(chips, *refs), out_shape=(jax.S...  254 us

profile of v2, /device:TPU:0, one launch (start us, length us, event | category | flops | bytes accessed | tf_op | source)
XLA Modules:
  0.0 259.0 jit_solution(12468813927959496402)
XLA Ops:
  0.6 1.3 reshape.17.refs_1_
  1.9 253.6 %fused.1 = (bf16[1024,224]{1,0:T(8,128)(2,1)}, f32[8,128]{1,0:T(8,128)}) custom-call(bf16[2,64,1792]{2,1,0:T(8,128)(2,1)} %bitcast.4, bf16[1,3584]{1,0:T(2,128)(2,1)} %reshape.17.refs_1_, bf16[224,5120]{1,0:T(8,128)(2,1)} %refs_2_.1, bf16[224,5120]{1,0:T(8,128)(2,1)} %refs_3_.1, bf16[224,5120]{1,0:T(8,128)(2,1)} %refs_4_.1, bf16[2,224,5120]{2,1,0:T(8,128)(2,1)} %refs_5_.1), custom_call_target="tpu_custom_call" | custom-call | tf_op jit(solution)/shard_map/fused/pallas_call | solution.py:428
  255.5 2.0 copy.10
  257.5 0.7 reshape.18
  258.3 0.7 reshape.19
  (1 shorter events, 0.0 us)

commit v3 on v2

--- a/solution.py
+++ b/solution.py
@@ -53,27 +53,27 @@
     pl.semaphore_signal(barrier, inc=1, device_id=across, device_id_type=MESH)
     pl.semaphore_wait(barrier, devices)
 
-    def token_slot(half, owner):
-        return tok.at[owner, :, :, pl.ds(pl.multiple_of(half * t_cols, 128), t_cols)]
-
-    def token_copy(src, half, owner, way, device):
-        return remote(src, token_slot(half, owner), t_send.at[way, owner], t_recv.at[half, owner], device)
-
-    def pass_on(src, owner, first):
+    def token_slot(half, owner, part):
+        return tok.at[owner, part, :, pl.ds(pl.multiple_of(half * t_cols, 128), t_cols)]
+
+    def token_copy(src, half, owner, part, way, device):
+        return remote(src, token_slot(half, owner, part), t_send.at[way, owner, part], t_recv.at[half, owner, part], device)
+
+    def pass_on(src, owner, part, first):
         if first in (0, 1):
             @pl.when(outer > 0)
             def _():
-                token_copy(src, tp, owner, 0, down).start()
+                token_copy(src, tp, owner, part, 0, down).start()
         if first in (0, 2):
             @pl.when(outer < outers - 1)
             def _():
-                token_copy(src, tp, owner, 1, up).start()
-        token_copy(src, tp, owner, 2, side).start()
-        token_copy(src, tp, owner, 3, across).start()
-
-    def token_wait(half, owner):
-        slot = token_slot(half, owner)
-        remote(slot, slot, t_send.at[3, owner], t_recv.at[half, owner], across).wait_recv()
+                token_copy(src, tp, owner, part, 1, up).start()
+        token_copy(src, tp, owner, part, 2, side).start()
+        token_copy(src, tp, owner, part, 3, across).start()
+
+    def token_wait(half, owner, part):
+        slot = token_slot(half, owner, part)
+        remote(slot, slot, t_send.at[3, owner, part], t_recv.at[half, owner, part], across).wait_recv()
 
     weights = (g_ref, u_ref)
 
@@ -111,14 +111,15 @@
             line(chip, -1, start_send)
             line(side_chip, -1, start_send)
 
-    pass_on(t_ref, chip, 0)
+    for part in range(parts):
+        pass_on(t_ref.at[part], chip, part, 0)
     for a in range(2):
         start_send(a, side_chip)
     weights_along(0)
     own_out = [remote(piece(a, chip), landing(a, chip, core), wc_send.at[a, chip], wc_recv.at[a, chip], partner) for a in range(2)]
     locals_ = [pltpu.make_async_copy(piece(a, chip), landing(a, chip, core), local_sem.at[a]) for a in range(2)]
     locals_ += [
-        pltpu.make_async_copy(t_ref, token_slot(tp, chip), local_sem.at[2]),
+        pltpu.make_async_copy(t_ref, tok.at[chip, :, :, pl.ds(pl.multiple_of(tp * t_cols, 128), t_cols)], local_sem.at[2]),
         pltpu.make_async_copy(m0_ref, mats.at[0], local_sem.at[3]),
         pltpu.make_async_copy(mp_ref, mats.at[pl.ds(1, kinds - 1)], local_sem.at[4]),
     ]
@@ -129,21 +130,24 @@
         @pl.when(outer - r >= 0)
         def _():
             owner = chip - 2 * r
-            token_wait(tp, owner)
-            pass_on(token_slot(tp, owner), owner, 2)
+            for part in range(parts):
+                token_wait(tp, owner, part)
+                pass_on(token_slot(tp, owner, part), owner, part, 2)
 
         @pl.when(outer + r < outers)
         def _():
             owner = chip + 2 * r
-            token_wait(tp, owner)
-            pass_on(token_slot(tp, owner), owner, 1)
+            for part in range(parts):
+                token_wait(tp, owner, part)
+                pass_on(token_slot(tp, owner, part), owner, part, 1)
 
         weights_along(r)
 
     for z in range(outers):
         owner = z * 2 + 1 - inner
-        token_wait(tp, owner)
-        token_copy(token_slot(tp, owner), tp, owner, 3, across).start()
+        for part in range(parts):
+            token_wait(tp, owner, part)
+            token_copy(token_slot(tp, owner, part), tp, owner, part, 3, across).start()
 
     def take(a, source):
         block = landing(a, source, core)
@@ -166,15 +170,13 @@
     def hidden(k):
         o, s = k // parts, k % parts
 
-        @pl.when(s == 0)
-        def _():
-            token_wait(1 - tp, o)
-            token_wait(1 - tp, owners + o)
+        for half in range(2):
+            token_wait(1 - tp, half * owners + o, s)
 
         def normed(owner):
             widened = tok[owner, s].astype(jnp.float32)
             inverse_rms = lax.rsqrt(jnp.mean(widened * widened, axis=1, keepdims=True) + epsilon)
-            return (widened * inverse_rms * gain_ref[...].astype(jnp.float32)).astype(jnp.bfloat16)
+            return (widened * inverse_rms * gain_ref[...].astype(jnp.float32)[None, :]).astype(jnp.bfloat16)
 
         left = jnp.concatenate([normed(o), normed(owners + o)], axis=0)
         sums = jnp.dot(left, wts[...].reshape(features, 2 * width), preferred_element_type=jnp.float32)
@@ -254,26 +256,32 @@
     def to_across(k):
         return remote(theirs.at[k], other.at[k], y_send.at[k], y_recv.at[k], across)
 
-    def finish(k):
-        for j in range(chips):
-            block = hall.at[k, j, 1 - core]
-            remote(block, block, c_send.at[k, j], c_recv.at[k, j], partner).wait_recv()
-        acc[...] = jnp.zeros_like(acc)
-
-        @pl.loop(0, chips // 2)
-        def _(p):
-            right = jnp.concatenate(
-                [jnp.concatenate([hall[k, 2 * p, c, half], hall[k, 2 * p + 1, c, half]], axis=1) for half in range(2) for c in range(2)],
-                axis=0,
-            )
-            left = mats[:, :, pl.ds(pl.multiple_of(p * 2 * width, 128), 2 * width)].reshape(kinds * col_width, 2 * width)
-            acc[...] += lax.dot_general(left, right, (((1,), (1,)), ((), ())), preferred_element_type=jnp.float32)
-
+    def gather(k, d):
+        def one(z):
+            @pl.when((z >= 0) & (z < outers))
+            def _():
+                pair = (2 * z, 2 * z + 1)
+                for j in pair:
+                    block = hall.at[k, j, 1 - core]
+                    remote(block, block, c_send.at[k, j], c_recv.at[k, j], partner).wait_recv()
+                right = jnp.concatenate(
+                    [jnp.concatenate([hall[k, j, c, half] for j in pair], axis=1) for half in range(2) for c in range(2)],
+                    axis=0,
+                )
+                left = mats[:, :, pl.ds(pl.multiple_of(z * 2 * width, 128), 2 * width)].reshape(kinds * col_width, 2 * width)
+                product = lax.dot_general(left, right, (((1,), (1,)), ((), ())), preferred_element_type=jnp.float32)
+                acc[k] = product if d == 0 else acc[k] + product
+
+        one(outer - d)
+        if d:
+            one(outer + d)
+
+    def deliver(k):
         def lanes(half):
             return pl.ds(pl.multiple_of(half * 2 * t_rows, 128), 2 * t_rows)
 
-        theirs[k] = acc[:, lanes(1 - tp)].astype(jnp.bfloat16)
-        mine[k] = acc[:, lanes(tp)].astype(jnp.bfloat16)
+        theirs[k] = acc[k, :, lanes(1 - tp)].astype(jnp.bfloat16)
+        mine[k] = acc[k, :, lanes(tp)].astype(jnp.bfloat16)
         to_across(k).start()
 
     def conclude(k):
@@ -307,6 +315,11 @@
             hidden(i)
             inject(i)
 
+        for d in range(outers - 1):
+            @pl.when((i - d - 2 >= 0) & (i - d - 2 < count))
+            def _():
+                gather(i - d - 2, d)
+
         for r in range(1, outers):
             @pl.when((i - r >= 0) & (i - r < count))
             def _():
@@ -320,7 +333,8 @@
 
         @pl.when((i - lag >= 0) & (i - lag < count))
         def _():
-            finish(i - lag)
+            gather(i - lag, outers - 1)
+            deliver(i - lag)
 
         @pl.when((i - lag - 1 >= 0) & (i - lag - 1 < count))
         def _():
@@ -351,8 +365,9 @@
                 weight_pass(a, s).wait_send()
 
     def sent(owner, way):
-        slot = token_slot(tp, owner)
-        remote(slot, slot, t_send.at[way, owner], t_recv.at[tp, owner], across).wait_send()
+        for part in range(parts):
+            slot = token_slot(tp, owner, part)
+            remote(slot, slot, t_send.at[way, owner, part], t_recv.at[tp, owner, part], across).wait_send()
 
     for s in range(chips):
         sent(s, 3)
@@ -408,7 +423,11 @@
     for d in range(1, devices):
         curve((me + devices - d) % devices, d).wait_recv()
         curve(me, d).wait_send()
-    curv_ref[...] = jnp.sum(curves[...], axis=0) / (PROBES * D)
+    totals = jnp.sum(curves[...], axis=0) / (PROBES * D)
+    for o in range(owners):
+        for c in range(2):
+            row = [totals[o * parts + s : o * parts + s + 1, c * t_rows : (c + 1) * t_rows] for s in range(parts)]
+            curv_ref[pl.ds(o * 2 + c, 1), :] = jnp.concatenate(row, axis=1)
 
 
 def fused(tokens, norm_gain, gate_weight, up_weight, down_weight, probes, chips):
@@ -427,7 +446,7 @@
     vmem = pl.BlockSpec(memory_space=pltpu.VMEM)
     out, curv = pl.pallas_call(
         lambda *refs: fused_kernel(chips, *refs),
-        out_shape=(jax.ShapeDtypeStruct((kept, col_width), jnp.bfloat16), jax.ShapeDtypeStruct((count, 2 * t_rows), jnp.float32)),
+        out_shape=(jax.ShapeDtypeStruct((kept, col_width), jnp.bfloat16), jax.ShapeDtypeStruct((chips, t_all), jnp.float32)),
         in_specs=[ANY, vmem, ANY, ANY, ANY, ANY],
         out_specs=[vmem] * 2,
         scratch_shapes=[
@@ -435,13 +454,13 @@
             pltpu.VMEM((chips, 2, rows, 2 * width), jnp.bfloat16),
             pltpu.VMEM((count, chips, 2, 2, t_rows, width), jnp.bfloat16),
             pltpu.VMEM((kinds, col_width, span), jnp.bfloat16),
-            pltpu.VMEM((kinds * col_width, 4 * t_rows), jnp.float32),
+            pltpu.VMEM((count, kinds * col_width, 4 * t_rows), jnp.float32),
             part,
             part,
             part,
             pltpu.VMEM((2 * chips, count, 2 * t_rows), jnp.float32),
-            pltpu.SemaphoreType.DMA((4, chips)),
-            pieces,
+            pltpu.SemaphoreType.DMA((4, chips, parts)),
+            pltpu.SemaphoreType.DMA((2, chips, parts)),
             pieces,
             pieces,
             pieces,
@@ -459,8 +478,7 @@
         ],
         compiler_params=pltpu.CompilerParams(collective_id=1, has_side_effects=True, vmem_limit_bytes=63 * 2**20),
         name="fused",
-    )(tokens.reshape(parts, t_rows, t_cols), norm_gain.reshape(1, -1), gate_weight, up_weight, down_weight, probes)
-    curv = curv.reshape(count // parts, parts, 2, t_rows).transpose(0, 2, 1, 3)
+    )(tokens.reshape(parts, t_rows, t_cols), norm_gain, gate_weight, up_weight, down_weight, probes)
     return out, curv.reshape(kept)
 
 

time: 259 us -> 255 us (0.985)
  Pallas kernels: 254 us -> 250 us
    pallas_call x1, Pallas kernels: 254 us -> 250 us  [fused(): pl.pallas_call(lambda *refs: fused_kernel(chips, *refs), out_shape=(jax.S...]
    reshape x4 -> x0, local copies, waits for them, and re-layouts: 2.73 us -> none  [the longest x1 1.31 us: fused(): norm_gain.reshape(1, -1)]
where the time goes in v3:
time: 255 us; the launch traced here: 254 us
  Pallas kernels  250 us (98%)
  local copies, waits for them, and re-layouts  3.27 us (1%)
    pallas_call x1, Pallas kernels, fused(): pl.pallas_call(lambda *refs: fused_kernel(chips, *refs), out_shape=(jax.S...  250 us

profile of v3, /device:TPU:0, one launch (start us, length us, event | category | flops | bytes accessed | tf_op | source)
XLA Modules:
  0.0 254.4 jit_solution(13752651081585262814)
XLA Ops:
  0.6 250.5 %fused.1 = (bf16[1024,224]{1,0:T(8,128)(2,1)}, f32[8,128]{1,0:T(8,128)}) custom-call(bf16[2,64,1792]{2,1,0:T(8,128)(2,1)} %bitcast.2, bf16[3584]{0:T(1024)(128)(2,1)} %refs_1_.1, bf16[224,5120]{1,0:T(8,128)(2,1)} %refs_2_.1, bf16[224,5120]{1,0:T(8,128)(2,1)} %refs_3_.1, bf16[224,5120]{1,0:T(8,128)(2,1)} %refs_4_.1, bf16[2,224,5120]{2,1,0:T(8,128)(2,1)} %refs_5_.1), custom_call_target="tpu_custom_call" | custom-call | tf_op jit(solution)/shard_map/fused/pallas_call | solution.py:447
  251.1 2.0 copy.8
  253.1 1.3 copy.10

commit v4 on v3

--- a/solution.py
+++ b/solution.py
@@ -306,7 +306,7 @@
             span = pl.ds(pl.multiple_of(((o * 2 + c) * parts + s) * t_rows, t_rows), t_rows)
             out_ref[span, :] = turned[c * t_rows : (c + 1) * t_rows, :col_width]
 
-    lag = outers
+    lag = outers + 1
 
     @pl.loop(0, count + lag)
     def _(i):
@@ -316,20 +316,20 @@
             inject(i)
 
         for d in range(outers - 1):
+            @pl.when((i - d - 3 >= 0) & (i - d - 3 < count))
+            def _():
+                gather(i - d - 3, d)
+
+        for r in range(1, outers):
+            @pl.when((i - r - 1 >= 0) & (i - r - 1 < count))
+            def _():
+                hop(i - r - 1, r, 0)
+                hop(i - r - 1, r, 1)
+
+        for d in range(outers):
             @pl.when((i - d - 2 >= 0) & (i - d - 2 < count))
             def _():
-                gather(i - d - 2, d)
-
-        for r in range(1, outers):
-            @pl.when((i - r >= 0) & (i - r < count))
-            def _():
-                hop(i - r, r, 0)
-                hop(i - r, r, 1)
-
-        for d in range(outers):
-            @pl.when((i - d - 1 >= 0) & (i - d - 1 < count))
-            def _():
-                beside(i - d - 1, d)
+                beside(i - d - 2, d)
 
         @pl.when((i - lag >= 0) & (i - lag < count))
         def _():

time: 255 us -> 253 us (level)
  no operation moved by 1% of the time
where the time goes in v4:
time: 253 us
  Pallas kernels  249 us (98%)
  local copies, waits for them, and re-layouts  3.27 us (1%)
    pallas_call x1, Pallas kernels, fused(): pl.pallas_call(lambda *refs: fused_kernel(chips, *refs), out_shape=(jax.S...  249 us

profile of v4, /device:TPU:0, one launch (start us, length us, event | category | flops | bytes accessed | tf_op | source)
XLA Modules:
  0.0 253.0 jit_solution(9930103846897585540)
XLA Ops:
  0.6 249.1 %fused.1 = (bf16[1024,224]{1,0:T(8,128)(2,1)}, f32[8,128]{1,0:T(8,128)}) custom-call(bf16[2,64,1792]{2,1,0:T(8,128)(2,1)} %bitcast.2, bf16[3584]{0:T(1024)(128)(2,1)} %refs_1_.1, bf16[224,5120]{1,0:T(8,128)(2,1)} %refs_2_.1, bf16[224,5120]{1,0:T(8,128)(2,1)} %refs_3_.1, bf16[224,5120]{1,0:T(8,128)(2,1)} %refs_4_.1, bf16[2,224,5120]{2,1,0:T(8,128)(2,1)} %refs_5_.1), custom_call_target="tpu_custom_call" | custom-call | tf_op jit(solution)/shard_map/fused/pallas_call | solution.py:447
  249.7 2.0 copy.8
  251.7 1.3 copy.10
